TPU v7x, 512 devices: a whole 4x8x8 slice. The times are simulated.
512 devices in a mesh: prow: 8 (over z), pcol: 64 (over y, x, core).
Axes of the slice: x: 4, y: 8, z: 8, core: 2. Of those that a mesh axis runs over, the one named last changes fastest.
Arguments:
- vectors: float32 [32768, 8192], P('prow', 'pcol'), may hold values from -6 to 6
- reflectors: bfloat16 [4, 256, 32768], P(None, 'pcol', 'prow'), may hold values from -0.03125 to 0.03125
- tau_diag: float32 [4, 256], replicated, may hold values from 0.5 to 1.5
- coupling: float32 [4, 256, 256], replicated, may hold values from -0.375 to 0.375
Outputs:
- result: float32 [32768, 8192], P('prow', 'pcol')
All inputs are finite; a program needn't handle non-finite values.
Results may differ from a plain program's by a relative error of at most 0.0003.
Values may be sent and summed in bfloat16 or wider, within the bound.
No kernel may reach another device: no remote copies, remote signals or barrier semaphores. Data moves between devices by JAX's collectives and lax.ppermute only.
A program may use at most 64 MiB of HBM per device.

v0:
```python
import jax
import jax.numpy as jnp
from jax import lax
from jax.sharding import Mesh
from jax.sharding import PartitionSpec as P

PCOL = ("pcol_0", "pcol_1", "pcol_2")


def joined_along(parts, dim):
    lengths = list(parts.shape[1:])
    lengths[dim] *= parts.shape[0]
    return jnp.moveaxis(parts, 0, dim).reshape(lengths)


def stacked_from(x, axes, sequence):
    parts = x[None]
    for k in sequence:
        parts = lax.all_gather(parts, axes[k], axis=0, tiled=True)
    carried = [lax.axis_size(axes[k]) for k in reversed(sequence)]
    parts = parts.reshape(*carried, *x.shape)
    turned = sorted(range(len(sequence)), key=lambda place: sequence[len(sequence) - 1 - place])
    return parts.transpose(*turned, *range(len(sequence), parts.ndim)).reshape(-1, *x.shape)


def gather_axes(x, axes, sequence, dim):
    return joined_along(stacked_from(x, axes, sequence), dim)


def in_blocks(x, dim, devices):
    lengths = x.shape
    parts = x.reshape(*lengths[:dim], devices, lengths[dim] // devices, *lengths[dim + 1 :])
    return jnp.moveaxis(parts, dim, 0)


def sum_at_owner(x, axis, dim):
    parts = in_blocks(x, dim, lax.axis_size(axis))
    arrived = lax.all_to_all(parts, axis, split_axis=0, concat_axis=0, tiled=True)
    return arrived.sum(axis=0)


def copy_for_each(x, axis):
    copies = jnp.broadcast_to(x, (lax.axis_size(axis), *x.shape))
    return lax.all_to_all(copies, axis, split_axis=0, concat_axis=0, tiled=True)


def gather_directly(x, axis, dim):
    return joined_along(copy_for_each(x, axis), dim)


def on_device(vectors, reflectors, tau_diag, coupling):
    count = reflectors.shape[0]
    gathered = gather_axes(reflectors, PCOL, (1, 0, 2), 1)
    current = vectors
    for position in range(count - 1, -1, -1):
        rows_panel = gathered[position]
        widened = rows_panel.astype(jnp.float32)
        tri_factor = jnp.diag(tau_diag[position]) + jnp.triu(coupling[position], 1)
        partial_sum = jnp.dot(
            widened, current, precision=lax.Precision.HIGHEST, preferred_element_type=jnp.float32
        )
        shares = sum_at_owner(partial_sum, "prow", 1)
        local_image = jnp.dot(
            tri_factor, shares, precision=lax.Precision.HIGHEST, preferred_element_type=jnp.float32
        )
        updates = gather_directly(local_image, "prow", 1)
        current = current - lax.dot_general(
            widened,
            updates,
            (((0,), (0,)), ((), ())),
            precision=lax.Precision.HIGHEST,
            preferred_element_type=jnp.float32,
        )
    return current


def solution(mesh):
    finer = Mesh(
        mesh.devices.reshape(mesh.shape["prow"], 8, 4, 2), ("prow", "pcol_0", "pcol_1", "pcol_2")
    )
    placed = (P("prow", PCOL), P(None, PCOL, "prow"), P(), P())
    return jax.shard_map(
        on_device, mesh=finer, in_specs=placed, out_specs=P("prow", PCOL), check_vma=False
    )
```

profile of v0, /device:TPU:2, one launch (start us, length us, event | category | flops | bytes accessed | tf_op | source)
XLA Modules:
  0.0 267.3 jit_solution(2077051281151391013)
XLA Ops:
  6.5 18.3 %all-gather = bf16[16,4,4096]{2,1,0:T(4,128)(2,1)} all-gather(bf16[4,4,4096]{2,1,0:T(4,128)(2,1)} %param.5), channel_id=2, replica_groups=mesh['prow'=8,'pcol_0'=8,'pcol_1'=4,'pcol_2'=2] {'pcol_1'}, dimensions={0}, use_global_device_ids=true | all-gather | bytes 655360 | tf_op jit(solution)/shard_map/all_gather | solution.py:19
  24.9 57.0 %all-gather.4.cloned.1.call-done = bf16[32,4,4,4096]{3,2,1,0:T(4,128)(2,1)} async-done(((bf16[4,4,4,4096]{3,2,1,0:T(4,128)(2,1)}), bf16[32,4,4,4096]{3,2,1,0:T(4,128)(2,1)}) %all-gather.4.cloned.1.call-update) | async-done | bytes 4194320 | tf_op jit(solution)/shard_map/all_gather | solution.py:19
  83.8 27.2 %all-gather.6.cloned.1.call-done = bf16[64,4,4,4096]{3,2,1,0:T(4,128)(2,1)} async-done(((bf16[32,4,4,4096]{3,2,1,0:T(4,128)(2,1)}), bf16[64,4,4,4096]{3,2,1,0:T(4,128)(2,1)}) %all-gather.6.cloned.1.call-update) | async-done | bytes 8388624 | tf_op jit(solution)/shard_map/all_gather | solution.py:19
  111.0 5.6 %copy.18 = bf16[8,4,2,4,4,4096]{5,4,3,2,1,0:T(4,128)(2,1)S(1)} copy(bf16[8,4,2,4,4,4096]{5,4,3,1,0,2:T(4,128)(2,1)} %bitcast.111) | data formatting | bytes 16777216 | tf_op jit(solution)/shard_map/transpose | solution.py:23
  116.6 5.4 %fusion.36 = (bf16[1,64,4,4096]{3,2,0,1:T(4,128)(2,1)}, bf16[1,64,4,4096]{3,2,0,1:T(4,128)(2,1)}, bf16[1,64,4,4096]{3,2,0,1:T(4,128)(2,1)}, bf16[1,64,4,4096]{3,2,0,1:T(4,128)(2,1)}) fusion(bf16[4,64,4,4096]{3,2,0,1:T(4,128)(2,1)S(1)} %bitcast.109), kind=kLoop, calls=%fused_computation.43 | loop fusion | bytes 16777216 | tf_op jit(solution)/shard_map/slice | solution.py:56
  122.1 4.0 %reshape.56 = bf16[256,4096,1]{1,0,2:T(8,128)(2,1)} reshape(bf16[1,64,4,4096]{3,2,0,1:T(4,128)(2,1)} %get-tuple-element.8) | data formatting | bytes 4194304 | tf_op jit(solution)/shard_map/squeeze | solution.py:56
  126.1 4.6 %convolution_bitcast_fusion.4 = f32[8,256,16]{1,2,0:T(8,128)} fusion(bf16[256,4096,1]{1,0,2:T(8,128)(2,1)} %reshape.56, f32[8,16,4096]{2,1,0:T(8,128)S(1)} %bitcast.110), kind=kOutput, calls=%fused_computation.8 | convolution fusion | flops 1610612736 | bytes 4325376 | tf_op jit(solution)/shard_map/dot_general | solution.py:59
  130.6 7.4 %all-to-all-start = ((f32[8,256,16]{1,2,0:T(8,128)}), f32[8,256,16]{1,2,0:T(8,128)S(1)}, u32[]{:S(2)}, u32[]{:S(2)}) async-start(f32[8,256,16]{1,2,0:T(8,128)} %convolution_bitcast_fusion.4), calls=%async_computation | async-start | bytes 262144 | tf_op jit(solution)/shard_map/all_to_all | solution.py:38
  138.0 9.5 %all-to-all-done = f32[8,256,16]{1,2,0:T(8,128)S(1)} async-done(((f32[8,256,16]{1,2,0:T(8,128)}), f32[8,256,16]{1,2,0:T(8,128)S(1)}, u32[]{:S(2)}, u32[]{:S(2)}) %all-to-all-start) | async-done | bytes 131104 | tf_op jit(solution)/shard_map/all_to_all | solution.py:38
  148.6 3.4 %all-to-all-start.1 = ((f32[8,256,16]{1,2,0:T(8,128)}), f32[8,256,16]{1,2,0:T(8,128)S(1)}, u32[]{:S(2)}, u32[]{:S(2)}) async-start(f32[8,256,16]{1,2,0:T(8,128)} %broadcast_in_dim.71), calls=%async_computation.1 | async-start | bytes 262144 | tf_op jit(solution)/shard_map/all_to_all | solution.py:44
  152.0 4.0 %squeeze.29 = bf16[256,4096]{1,0:T(8,128)(2,1)} reshape(bf16[1,64,4,4096]{3,2,0,1:T(4,128)(2,1)} %get-tuple-element.8) | data formatting | bytes 4194304 | tf_op jit(solution)/shard_map/squeeze | solution.py:56
  156.0 3.9 %squeeze.31 = bf16[256,4096]{1,0:T(8,128)(2,1)} reshape(bf16[1,64,4,4096]{3,2,0,1:T(4,128)(2,1)} %get-tuple-element.7) | data formatting | bytes 4194304 | tf_op jit(solution)/shard_map/squeeze | solution.py:56
  166.1 15.0 %all_to_all.40 = f32[8,256,16]{1,2,0:T(8,128)S(1)} all-to-all(f32[8,256,16]{1,2,0:T(8,128)S(1)} %bitcast.117), channel_id=1, replica_groups=mesh['prow'=8,'pcol_0'=8,'pcol_1'=4,'pcol_2'=2] {'prow'}, dimensions={0} | all-to-all | bytes 262144 | tf_op jit(solution)/shard_map/all_to_all | solution.py:38
  182.1 3.4 %all-to-all-start.3 = ((f32[8,256,16]{1,2,0:T(8,128)}), f32[8,256,16]{1,2,0:T(8,128)S(1)}, u32[]{:S(2)}, u32[]{:S(2)}) async-start(f32[8,256,16]{1,2,0:T(8,128)} %broadcast_in_dim.74), calls=%async_computation.3 | async-start | bytes 262144 | tf_op jit(solution)/shard_map/all_to_all | solution.py:44
  187.6 6.9 %all-to-all-done.3 = f32[8,256,16]{1,2,0:T(8,128)S(1)} async-done(((f32[8,256,16]{1,2,0:T(8,128)}), f32[8,256,16]{1,2,0:T(8,128)S(1)}, u32[]{:S(2)}, u32[]{:S(2)}) %all-to-all-start.3) | async-done | bytes 131104 | tf_op jit(solution)/shard_map/all_to_all | solution.py:44
  194.5 3.4 %fusion.2 = f32[4096,128]{0,1:T(8,128)S(1)} fusion(f32[4096,128]{0,1:T(8,128)} %copy-done, f32[256,128]{0,1:T(8,128)S(1)} %bitcast.115, bf16[256,4096]{1,0:T(8,128)(2,1)} %squeeze.31), kind=kOutput, calls=%fused_computation.5 | convolution fusion | flops 1611137024 | bytes 6422528 | tf_op jit(solution)/shard_map/dot_general | solution.py:67
  200.1 11.5 %all_to_all.41 = f32[8,256,16]{1,2,0:T(8,128)S(1)} all-to-all(f32[8,256,16]{1,2,0:T(8,128)S(1)} %bitcast.118), channel_id=1, replica_groups=mesh['prow'=8,'pcol_0'=8,'pcol_1'=4,'pcol_2'=2] {'prow'}, dimensions={0} | all-to-all | bytes 262144 | tf_op jit(solution)/shard_map/all_to_all | solution.py:38
  212.7 3.5 %all-to-all-start.5 = ((f32[8,256,16]{1,2,0:T(8,128)}), f32[8,256,16]{1,2,0:T(8,128)S(1)}, u32[]{:S(2)}, u32[]{:S(2)}) async-start(f32[8,256,16]{1,2,0:T(8,128)} %broadcast_in_dim.77), calls=%async_computation.5 | async-start | bytes 262144 | tf_op jit(solution)/shard_map/all_to_all | solution.py:44
  216.2 4.0 %squeeze.35 = bf16[256,4096]{1,0:T(8,128)(2,1)} reshape(bf16[1,64,4,4096]{3,2,0,1:T(4,128)(2,1)} %get-tuple-element.5) | data formatting | bytes 4194304 | tf_op jit(solution)/shard_map/squeeze | solution.py:56
  220.2 4.9 %all-to-all-done.5 = f32[8,256,16]{1,2,0:T(8,128)S(1)} async-done(((f32[8,256,16]{1,2,0:T(8,128)}), f32[8,256,16]{1,2,0:T(8,128)S(1)}, u32[]{:S(2)}, u32[]{:S(2)}) %all-to-all-start.5) | async-done | bytes 131104 | tf_op jit(solution)/shard_map/all_to_all | solution.py:44
  230.1 11.6 %all_to_all.42 = f32[8,256,16]{1,2,0:T(8,128)S(1)} all-to-all(f32[8,256,16]{1,2,0:T(8,128)S(1)} %bitcast.119), channel_id=1, replica_groups=mesh['prow'=8,'pcol_0'=8,'pcol_1'=4,'pcol_2'=2] {'prow'}, dimensions={0} | all-to-all | bytes 262144 | tf_op jit(solution)/shard_map/all_to_all | solution.py:38
  242.2 11.5 %all_to_all.43 = f32[8,256,16]{1,2,0:T(8,128)S(1)} all-to-all(f32[8,256,16]{1,2,0:T(8,128)S(1)} %broadcast_in_dim.80), channel_id=1, replica_groups=mesh['prow'=8,'pcol_0'=8,'pcol_1'=4,'pcol_2'=2] {'prow'}, dimensions={0} | all-to-all | bytes 262144 | tf_op jit(solution)/shard_map/all_to_all | solution.py:44
  253.6 3.9 %fusion = f32[4096,128]{0,1:T(8,128)} fusion(f32[4096,128]{0,1:T(8,128)} %copy-done.1, f32[256,128]{0,1:T(8,128)S(1)} %bitcast.116, bf16[256,4096]{1,0:T(8,128)(2,1)S(1)} %copy-done.5), kind=kOutput, calls=%fused_computation.1 | convolution fusion | flops 1611137024 | bytes 6422528 | tf_op jit(solution)/shard_map/dot_general | solution.py:67
  257.5 2.9 %copy.21 = f32[4096,128]{1,0:T(8,128)} copy(f32[4096,128]{0,1:T(8,128)} %fusion) | data formatting | bytes 4194304 | tf_op jit(solution)/shard_map/sub | solution.py:67
  (43 shorter events, 21.2 us)
Async XLA Ops:
  6.5 75.3 %all-gather.4.cloned.1.call-start = ((), (), s32[]{:S(2)}) async-start(), calls=%async_computation.8 | async-start | bytes 4718592 | tf_op jit(solution)/shard_map/all_gather | solution.py:19
  24.8 86.2 %all-gather.6.cloned.1.call-start = ((), (), s32[]{:S(2)}) async-start(), calls=%async_computation.9 | async-start | bytes 12582912 | tf_op jit(solution)/shard_map/all_gather | solution.py:19
  126.0 11.9 %copy-start.7 = (f32[4,256]{1,0:T(4,128)S(1)}, f32[4,256]{1,0:T(4,128)}, u32[]{:S(2)}) copy-start(f32[4,256]{1,0:T(4,128)} %param.6) | copy-start | bytes 12292
  126.0 21.5 %copy-start.8 = (f32[4,256,256]{2,1,0:T(8,128)S(1)}, f32[4,256,256]{2,1,0:T(8,128)}, u32[]{:S(2)}) copy-start(f32[4,256,256]{2,1,0:T(8,128)} %param.7) | copy-start | bytes 3145732
  130.6 16.9 %all-to-all-start = ((f32[8,256,16]{1,2,0:T(8,128)}), f32[8,256,16]{1,2,0:T(8,128)S(1)}, u32[]{:S(2)}, u32[]{:S(2)}) async-start(f32[8,256,16]{1,2,0:T(8,128)} %convolution_bitcast_fusion.4), calls=%async_computation | async-start | bytes 262144 | tf_op jit(solution)/shard_map/all_to_all | solution.py:38
  148.6 12.4 %all-to-all-start.1 = ((f32[8,256,16]{1,2,0:T(8,128)}), f32[8,256,16]{1,2,0:T(8,128)S(1)}, u32[]{:S(2)}, u32[]{:S(2)}) async-start(f32[8,256,16]{1,2,0:T(8,128)} %broadcast_in_dim.71), calls=%async_computation.1 | async-start | bytes 262144 | tf_op jit(solution)/shard_map/all_to_all | solution.py:44
  161.0 2.9 %copy-start.3 = (bf16[256,4096]{1,0:T(8,128)(2,1)S(1)}, bf16[256,4096]{1,0:T(8,128)(2,1)}, u32[]{:S(2)}) copy-start(bf16[256,4096]{1,0:T(8,128)(2,1)} %squeeze.31) | copy-start | bytes 6291460
  163.8 2.2 copy-start
  163.9 21.7 %copy-start.6 = (bf16[1,64,4,4096]{3,2,0,1:T(4,128)(2,1)S(1)}, bf16[1,64,4,4096]{3,2,0,1:T(4,128)(2,1)}, u32[]{:S(2)}) copy-start(bf16[1,64,4,4096]{3,2,0,1:T(4,128)(2,1)} %get-tuple-element.6) | copy-start | bytes 6291460
  182.1 12.4 %all-to-all-start.3 = ((f32[8,256,16]{1,2,0:T(8,128)}), f32[8,256,16]{1,2,0:T(8,128)S(1)}, u32[]{:S(2)}, u32[]{:S(2)}) async-start(f32[8,256,16]{1,2,0:T(8,128)} %broadcast_in_dim.74), calls=%async_computation.3 | async-start | bytes 262144 | tf_op jit(solution)/shard_map/all_to_all | solution.py:44
  194.5 3.4 %copy-start.2 = (bf16[256,4096]{1,0:T(8,128)(2,1)S(1)}, bf16[256,4096]{1,0:T(8,128)(2,1)}, u32[]{:S(2)}) copy-start(bf16[256,4096]{1,0:T(8,128)(2,1)} %squeeze.33) | copy-start | bytes 6291460
  212.7 12.4 %all-to-all-start.5 = ((f32[8,256,16]{1,2,0:T(8,128)}), f32[8,256,16]{1,2,0:T(8,128)S(1)}, u32[]{:S(2)}, u32[]{:S(2)}) async-start(f32[8,256,16]{1,2,0:T(8,128)} %broadcast_in_dim.77), calls=%async_computation.5 | async-start | bytes 262144 | tf_op jit(solution)/shard_map/all_to_all | solution.py:44
  225.0 2.9 %copy-start.4 = (bf16[256,4096]{1,0:T(8,128)(2,1)S(1)}, bf16[256,4096]{1,0:T(8,128)(2,1)}, u32[]{:S(2)}) copy-start(bf16[256,4096]{1,0:T(8,128)(2,1)} %squeeze.35) | copy-start | bytes 6291460
  227.9 2.3 copy-start.1
  227.9 25.7 %copy-start.5 = (bf16[256,4096]{1,0:T(8,128)(2,1)S(1)}, bf16[256,4096]{1,0:T(8,128)(2,1)}, u32[]{:S(2)}) copy-start(bf16[256,4096]{1,0:T(8,128)(2,1)} %squeeze.35) | copy-start | bytes 6291460
Sparse Core Ops, SparseCore 0:
  24.9 56.8 all-gather.3
  84.0 27.0 all-gather.5
where the time goes:
time: 268 us; the launch traced here: 267 us
  waiting for transfers between devices  107 us (40%)
  blocking collectives  67.7 us (25%)
  local copies, waits for them, and re-layouts  36 us (13%)
  matrix products  25.6 us (10%)
  starting transfers between devices  17.7 us (7%)
  between operations  13.6 us (5%)
    all_gather x2, waiting for transfers between devices, stacked_from(): parts = lax.all_gather(parts, axes[k], axis=0, tiled=True)  84.2 us
    all_to_all x3, blocking collectives, sum_at_owner(): lax.all_to_all(parts, axis, split_axis=0, concat_axis=0, tiled=True)  38 us
    all_gather x1, blocking collectives, stacked_from(): parts = lax.all_gather(parts, axes[k], axis=0, tiled=True)  18.3 us
    squeeze x5, local copies, waits for them, and re-layouts, on_device(): rows_panel = gathered[position]  17.9 us
    dot_general x4, matrix products, on_device(): lax.dot_general(widened, updates, (((0,), (0,)), ((), ())), precision=lax...  12.9 us
    all_to_all x3, waiting for transfers between devices, copy_for_each(): return lax.all_to_all(copies, axis, split_axis=0, concat_axis=0, tiled=True)  12.8 us
    all_to_all x1, blocking collectives, copy_for_each(): return lax.all_to_all(copies, axis, split_axis=0, concat_axis=0, tiled=True)  11.5 us
    dot_general x4, matrix products, on_device(): jnp.dot(widened, current, precision=lax.Precision.HIGHEST, preferred_elem...  11.2 us
  transfers between devices with their start and end apart: 6, of which 6 were waited for; matrix products, arithmetic and copies ran while one was open for 6% of the time, Pallas kernels for 0%

commit v1 on v0

--- a/solution.py
+++ b/solution.py
@@ -16,7 +16,9 @@
 def stacked_from(x, axes, sequence):
     parts = x[None]
     for k in sequence:
-        parts = lax.all_gather(parts, axes[k], axis=0, tiled=True)
+        parts = jnp.concatenate(
+            lax.all_to_all(jnp.stack([parts] * lax.axis_size(axes[k])), axes[k], 0, 0), axis=0
+        )
     carried = [lax.axis_size(axes[k]) for k in reversed(sequence)]
     parts = parts.reshape(*carried, *x.shape)
     turned = sorted(range(len(sequence)), key=lambda place: sequence[len(sequence) - 1 - place])

time: 268 us -> 298 us (1.11)
  local copies, waits for them, and re-layouts: 36 us -> 52.8 us
  between operations: 13.6 us -> 0.24 us
  starting transfers between devices: 17.7 us -> 28.8 us
  other arithmetic: 0.05 us -> 7.94 us
  waiting for transfers between devices: 107 us -> 112 us
    all_to_all x0 -> x1, waiting for transfers between devices: none -> 93.4 us  [stacked_from(): lax.all_to_all(jnp.stack([parts] * lax.axis_size(axes[k])), axes[k], 0, 0)]
    all_gather x2 -> x0, waiting for transfers between devices: 84.2 us -> none  [stacked_from(): parts = lax.all_gather(parts, axes[k], axis=0, tiled=True)]
    all_gather x1 -> x0, blocking collectives: 18.3 us -> none  [stacked_from(): parts = lax.all_gather(parts, axes[k], axis=0, tiled=True)]
    all_to_all x1 -> x2, blocking collectives: 11.5 us -> 25.4 us  [stacked_from(): lax.all_to_all(jnp.stack([parts] * lax.axis_size(axes[k])), axes[k], 0, 0)]
    squeeze x5 -> x8, local copies, waits for them, and re-layouts: 17.9 us -> 30.3 us  [on_device(): rows_panel = gathered[position]]
    another operation x0 -> x3, local copies, waits for them, and re-layouts: none -> 9.42 us  [the longest x2 5.17 us: stacked_from(): jnp.stack([parts] * lax.axis_size(axes[k]))]
    another operation x0 -> x1, other arithmetic: none -> 7.89 us  [stacked_from(): jnp.stack([parts] * lax.axis_size(axes[k]))]
    transpose x1 -> x0, local copies, waits for them, and re-layouts: 5.62 us -> none  [stacked_from(): parts.transpose(*turned, *range(len(sequence), parts.ndim))]
  transfers between devices with their start and end apart: 6 -> 6, of which waited for: 6 -> 6; matrix products, arithmetic and copies ran while one was open for 6% -> 10% of each run, Pallas kernels for 0% -> 0%
where the time goes in v1:
time: 298 us; the launch traced here: 296 us
  waiting for transfers between devices  112 us (38%)
  blocking collectives  68.5 us (23%)
  local copies, waits for them, and re-layouts  52.8 us (18%)
  starting transfers between devices  28.8 us (10%)
  matrix products  25.6 us (9%)
  other arithmetic  7.94 us (3%)
    all_to_all x1, waiting for transfers between devices, stacked_from(): lax.all_to_all(jnp.stack([parts] * lax.axis_size(axes[k])), axes[k], 0, 0)  93.4 us
    all_to_all x3, blocking collectives, sum_at_owner(): lax.all_to_all(parts, axis, split_axis=0, concat_axis=0, tiled=True)  43.2 us
    squeeze x8, local copies, waits for them, and re-layouts, on_device(): rows_panel = gathered[position]  30.3 us
    all_to_all x2, blocking collectives, stacked_from(): lax.all_to_all(jnp.stack([parts] * lax.axis_size(axes[k])), axes[k], 0, 0)  25.4 us
    all_to_all x4, starting transfers between devices, copy_for_each(): return lax.all_to_all(copies, axis, split_axis=0, concat_axis=0, tiled=True)  13.7 us
    dot_general x4, matrix products, on_device(): lax.dot_general(widened, updates, (((0,), (0,)), ((), ())), precision=lax...  13 us
    dot_general x4, matrix products, on_device(): jnp.dot(widened, current, precision=lax.Precision.HIGHEST, preferred_elem...  11.2 us
    all_to_all x1, starting transfers between devices, sum_at_owner(): lax.all_to_all(parts, axis, split_axis=0, concat_axis=0, tiled=True)  10.3 us
  transfers between devices with their start and end apart: 6, of which 6 were waited for; matrix products, arithmetic and copies ran while one was open for 10% of the time, Pallas kernels for 0%

profile of v1, /device:TPU:2, one launch (start us, length us, event | category | flops | bytes accessed | tf_op | source)
XLA Modules:
  0.0 296.2 jit_solution(2634276168764888323)
XLA Ops:
  1.1 14.9 %all_to_all.55 = bf16[4,1,4,4,4096]{4,3,2,1,0:T(4,128)(2,1)S(1)} all-to-all(bf16[4,1,4,4,4096]{4,3,2,1,0:T(4,128)(2,1)S(1)} %stack.9), channel_id=1, replica_groups=mesh['prow'=8,'pcol_0'=8,'pcol_1'=4,'pcol_2'=2] {'pcol_1'}, dimensions={0} | all-to-all | bytes 1048576 | tf_op jit(solution)/shard_map/all_to_all | solution.py:20
  16.0 4.1 %stack.10 = bf16[8,4,4,4,4096]{4,3,2,1,0:T(4,128)(2,1)} broadcast(bf16[4,4,4,4096]{3,2,1,0:T(4,128)(2,1)S(1)} %bitcast.106), dimensions={1,2,3,4} | broadcast | bytes 4718592 | tf_op jit(solution)/shard_map/stack | solution.py:20
  20.1 4.8 %all-to-all-start.1 = ((bf16[8,4,4,4,4096]{4,3,2,1,0:T(4,128)(2,1)}), bf16[8,4,4,4,4096]{4,3,2,1,0:T(4,128)(2,1)}, u32[]{:S(2)}, u32[]{:S(2)}) async-start(bf16[8,4,4,4,4096]{4,3,2,1,0:T(4,128)(2,1)} %stack.10), calls=%async_computation.1 | async-start | bytes 8388608 | tf_op jit(solution)/shard_map/all_to_all | solution.py:20
  26.9 93.4 %all-to-all-done.1 = bf16[8,4,4,4,4096]{4,3,2,1,0:T(4,128)(2,1)} async-done(((bf16[8,4,4,4,4096]{4,3,2,1,0:T(4,128)(2,1)}), bf16[8,4,4,4,4096]{4,3,2,1,0:T(4,128)(2,1)}, u32[]{:S(2)}, u32[]{:S(2)}) %all-to-all-start.1) | async-done | bytes 4194336 | tf_op jit(solution)/shard_map/all_to_all | solution.py:20
  120.2 7.9 %pad_maximum_fusion = bf16[2,32,4,4,4096]{4,3,2,1,0:T(4,128)(2,1)S(1)} fusion(bf16[1,32,4,4,4096]{4,3,2,1,0:T(4,128)(2,1)} %bitcast.1), kind=kLoop, calls=%fused_computation | loop fusion | flops 4194304 | bytes 12582912 | tf_op jit(solution)/shard_map/stack | solution.py:20
  128.1 10.5 %all_to_all.56 = bf16[2,32,4,4,4096]{4,3,2,1,0:T(4,128)(2,1)S(1)} all-to-all(bf16[2,32,4,4,4096]{4,3,2,1,0:T(4,128)(2,1)S(1)} %pad_maximum_fusion), channel_id=1, replica_groups=mesh['prow'=8,'pcol_0'=8,'pcol_1'=4,'pcol_2'=2] {'pcol_2'}, dimensions={0} | all-to-all | bytes 16777216 | tf_op jit(solution)/shard_map/all_to_all | solution.py:20
  138.6 4.2 %copy.21 = bf16[2,8,4,4,4,4096]{5,4,3,0,2,1:T(4,128)(2,1)S(1)} copy(bf16[2,8,4,4,4,4096]{5,4,3,2,1,0:T(4,128)(2,1)S(1)} %bitcast.101) | data formatting | bytes 16777216 | tf_op jit(solution)/shard_map/reshape;reshape | solution.py:23
  142.9 5.4 %fusion.32 = (bf16[1,64,4,4096]{3,2,0,1:T(4,128)(2,1)}, bf16[1,64,4,4096]{3,2,0,1:T(4,128)(2,1)}, bf16[1,64,4,4096]{3,2,0,1:T(4,128)(2,1)}, bf16[1,64,4,4096]{3,2,0,1:T(4,128)(2,1)}) fusion(bf16[4,64,4,4096]{3,2,0,1:T(4,128)(2,1)S(1)} %bitcast.100), kind=kLoop, calls=%fused_computation.43 | loop fusion | bytes 16777216 | tf_op jit(solution)/shard_map/slice | solution.py:58
  148.3 4.0 %reshape.49 = bf16[256,4096,1]{1,0,2:T(8,128)(2,1)} reshape(bf16[1,64,4,4096]{3,2,0,1:T(4,128)(2,1)} %get-tuple-element.8) | data formatting | bytes 4194304 | tf_op jit(solution)/shard_map/squeeze | solution.py:58
  152.3 4.6 %convolution_bitcast_fusion.3 = f32[8,256,16]{1,2,0:T(8,128)} fusion(bf16[256,4096,1]{1,0,2:T(8,128)(2,1)} %reshape.49, f32[8,16,4096]{2,1,0:T(8,128)S(1)} %bitcast.105), kind=kOutput, calls=%fused_computation.8 | convolution fusion | flops 1610612736 | bytes 4325376 | tf_op jit(solution)/shard_map/dot_general | solution.py:61
  156.8 10.3 %all-to-all-start.3 = ((f32[8,256,16]{1,2,0:T(8,128)}), f32[8,256,16]{1,2,0:T(8,128)S(1)}, u32[]{:S(2)}, u32[]{:S(2)}) async-start(f32[8,256,16]{1,2,0:T(8,128)} %convolution_bitcast_fusion.3), calls=%async_computation.3 | async-start | bytes 262144 | tf_op jit(solution)/shard_map/all_to_all | solution.py:40
  167.2 9.4 %all-to-all-done.3 = f32[8,256,16]{1,2,0:T(8,128)S(1)} async-done(((f32[8,256,16]{1,2,0:T(8,128)}), f32[8,256,16]{1,2,0:T(8,128)S(1)}, u32[]{:S(2)}, u32[]{:S(2)}) %all-to-all-start.3) | async-done | bytes 131104 | tf_op jit(solution)/shard_map/all_to_all | solution.py:40
  181.0 4.0 %squeeze.28 = bf16[256,4096]{1,0:T(8,128)(2,1)} reshape(bf16[1,64,4,4096]{3,2,0,1:T(4,128)(2,1)} %get-tuple-element.8) | data formatting | bytes 4194304 | tf_op jit(solution)/shard_map/squeeze | solution.py:58
  185.0 4.0 %reshape.50 = bf16[256,4096,1]{1,0,2:T(8,128)(2,1)} reshape(bf16[1,64,4,4096]{3,2,0,1:T(4,128)(2,1)} %get-tuple-element.7) | data formatting | bytes 4194304 | tf_op jit(solution)/shard_map/squeeze | solution.py:58
  195.1 15.0 %all_to_all.57 = f32[8,256,16]{1,2,0:T(8,128)S(1)} all-to-all(f32[8,256,16]{1,2,0:T(8,128)S(1)} %convolution_bitcast_fusion.2), channel_id=1, replica_groups=mesh['prow'=8,'pcol_0'=8,'pcol_1'=4,'pcol_2'=2] {'prow'}, dimensions={0} | all-to-all | bytes 262144 | tf_op jit(solution)/shard_map/all_to_all | solution.py:40
  211.2 3.5 %all-to-all-start.6 = ((f32[8,256,16]{1,2,0:T(8,128)}), f32[8,256,16]{1,2,0:T(8,128)S(1)}, u32[]{:S(2)}, u32[]{:S(2)}) async-start(f32[8,256,16]{1,2,0:T(8,128)} %broadcast_in_dim.70), calls=%async_computation.6 | async-start | bytes 262144 | tf_op jit(solution)/shard_map/all_to_all | solution.py:46
  214.8 4.2 %squeeze.30 = bf16[256,4096]{1,0:T(8,128)(2,1)} reshape(bf16[1,64,4,4096]{3,2,0,1:T(4,128)(2,1)} %get-tuple-element.7) | data formatting | bytes 4194304 | tf_op jit(solution)/shard_map/squeeze | solution.py:58
  229.2 13.2 %all_to_all.58 = f32[8,256,16]{1,2,0:T(8,128)S(1)} all-to-all(f32[8,256,16]{1,2,0:T(8,128)S(1)} %convolution_bitcast_fusion.1), channel_id=1, replica_groups=mesh['prow'=8,'pcol_0'=8,'pcol_1'=4,'pcol_2'=2] {'prow'}, dimensions={0} | all-to-all | bytes 262144 | tf_op jit(solution)/shard_map/all_to_all | solution.py:40
  246.9 4.0 %squeeze.32 = bf16[256,4096]{1,0:T(8,128)(2,1)} reshape(bf16[1,64,4,4096]{3,2,0,1:T(4,128)(2,1)} %get-tuple-element.6) | data formatting | bytes 4194304 | tf_op jit(solution)/shard_map/squeeze | solution.py:58
  250.9 3.9 %reshape.52 = bf16[256,4096,1]{1,0,2:T(8,128)(2,1)} reshape(bf16[1,64,4,4096]{3,2,0,1:T(4,128)(2,1)} %get-tuple-element.5) | data formatting | bytes 4194304 | tf_op jit(solution)/shard_map/squeeze | solution.py:58
  261.0 14.9 %all_to_all.59 = f32[8,256,16]{1,2,0:T(8,128)S(1)} all-to-all(f32[8,256,16]{1,2,0:T(8,128)S(1)} %convolution_bitcast_fusion), channel_id=1, replica_groups=mesh['prow'=8,'pcol_0'=8,'pcol_1'=4,'pcol_2'=2] {'prow'}, dimensions={0} | all-to-all | bytes 262144 | tf_op jit(solution)/shard_map/all_to_all | solution.py:40
  280.4 4.1 %squeeze.34 = bf16[256,4096]{1,0:T(8,128)(2,1)} reshape(bf16[1,64,4,4096]{3,2,0,1:T(4,128)(2,1)} %get-tuple-element.5) | data formatting | bytes 4194304 | tf_op jit(solution)/shard_map/squeeze | solution.py:58
  284.5 4.9 %all-to-all-done.10 = f32[8,256,16]{1,2,0:T(8,128)S(1)} async-done(((f32[8,256,16]{1,2,0:T(8,128)}), f32[8,256,16]{1,2,0:T(8,128)S(1)}, u32[]{:S(2)}, u32[]{:S(2)}) %all-to-all-start.10) | async-done | bytes 131104 | tf_op jit(solution)/shard_map/all_to_all | solution.py:46
  289.4 3.9 %convolution_subtract_fusion = f32[4096,128]{0,1:T(8,128)} fusion(f32[4096,128]{0,1:T(8,128)S(1)} %copy-done.1, bf16[256,4096]{1,0:T(8,128)(2,1)} %squeeze.34, f32[256,128]{0,1:T(8,128)S(1)} %bitcast.110), kind=kOutput, calls=%fused_computation.1 | convolution fusion | flops 1611137024 | bytes 6422528 | tf_op jit(solution)/shard_map/dot_general | solution.py:69
  (47 shorter events, 42.8 us)
Async XLA Ops:
  20.1 100.1 %all-to-all-start.1 = ((bf16[8,4,4,4,4096]{4,3,2,1,0:T(4,128)(2,1)}), bf16[8,4,4,4,4096]{4,3,2,1,0:T(4,128)(2,1)}, u32[]{:S(2)}, u32[]{:S(2)}) async-start(bf16[8,4,4,4,4096]{4,3,2,1,0:T(4,128)(2,1)} %stack.10), calls=%async_computation.1 | async-start | bytes 8388608 | tf_op jit(solution)/shard_map/all_to_all | solution.py:20
  152.3 14.9 %copy-start.7 = (f32[4,256]{1,0:T(4,128)S(1)}, f32[4,256]{1,0:T(4,128)}, u32[]{:S(2)}) copy-start(f32[4,256]{1,0:T(4,128)} %param.6) | copy-start | bytes 12292
  152.3 24.3 %copy-start.8 = (f32[4,256,256]{2,1,0:T(8,128)S(1)}, f32[4,256,256]{2,1,0:T(8,128)}, u32[]{:S(2)}) copy-start(f32[4,256,256]{2,1,0:T(8,128)} %param.7) | copy-start | bytes 3145732
  156.8 19.7 %all-to-all-start.3 = ((f32[8,256,16]{1,2,0:T(8,128)}), f32[8,256,16]{1,2,0:T(8,128)S(1)}, u32[]{:S(2)}, u32[]{:S(2)}) async-start(f32[8,256,16]{1,2,0:T(8,128)} %convolution_bitcast_fusion.3), calls=%async_computation.3 | async-start | bytes 262144 | tf_op jit(solution)/shard_map/all_to_all | solution.py:40
  177.6 12.4 %all-to-all-start.4 = ((f32[8,256,16]{1,2,0:T(8,128)}), f32[8,256,16]{1,2,0:T(8,128)S(1)}, u32[]{:S(2)}, u32[]{:S(2)}) async-start(f32[8,256,16]{1,2,0:T(8,128)} %broadcast_in_dim.67), calls=%async_computation.4 | async-start | bytes 262144 | tf_op jit(solution)/shard_map/all_to_all | solution.py:46
  190.0 2.9 copy-start.4
  192.9 2.3 copy-start.2
  211.2 12.4 %all-to-all-start.6 = ((f32[8,256,16]{1,2,0:T(8,128)}), f32[8,256,16]{1,2,0:T(8,128)S(1)}, u32[]{:S(2)}, u32[]{:S(2)}) async-start(f32[8,256,16]{1,2,0:T(8,128)} %broadcast_in_dim.70), calls=%async_computation.6 | async-start | bytes 262144 | tf_op jit(solution)/shard_map/all_to_all | solution.py:46
  214.8 4.2 %copy-start.3 = (bf16[1,64,4,4096]{3,2,0,1:T(4,128)(2,1)S(1)}, bf16[1,64,4,4096]{3,2,0,1:T(4,128)(2,1)}, u32[]{:S(2)}) copy-start(bf16[1,64,4,4096]{3,2,0,1:T(4,128)(2,1)} %get-tuple-element.6) | copy-start | bytes 6291460
  223.6 3.4 %copy-start.5 = (bf16[256,4096,1]{1,0,2:T(8,128)(2,1)S(1)}, bf16[256,4096,1]{1,0,2:T(8,128)(2,1)}, u32[]{:S(2)}) copy-start(bf16[256,4096,1]{1,0,2:T(8,128)(2,1)} %reshape.51) | copy-start | bytes 6291460
  243.5 12.4 %all-to-all-start.8 = ((f32[8,256,16]{1,2,0:T(8,128)}), f32[8,256,16]{1,2,0:T(8,128)S(1)}, u32[]{:S(2)}, u32[]{:S(2)}) async-start(f32[8,256,16]{1,2,0:T(8,128)} %broadcast_in_dim.73), calls=%async_computation.8 | async-start | bytes 262144 | tf_op jit(solution)/shard_map/all_to_all | solution.py:46
  255.9 2.9 copy-start.6
  258.8 2.3 copy-start
  277.0 12.4 %all-to-all-start.10 = ((f32[8,256,16]{1,2,0:T(8,128)}), f32[8,256,16]{1,2,0:T(8,128)S(1)}, u32[]{:S(2)}, u32[]{:S(2)}) async-start(f32[8,256,16]{1,2,0:T(8,128)} %broadcast_in_dim.76), calls=%async_computation.10 | async-start | bytes 262144 | tf_op jit(solution)/shard_map/all_to_all | solution.py:46
  280.4 9.0 %copy-start.1 = (f32[4096,128]{0,1:T(8,128)S(1)}, f32[4096,128]{0,1:T(8,128)}, u32[]{:S(2)}) copy-start(f32[4096,128]{0,1:T(8,128)} %copy-done) | copy-start | bytes 6291460
